TPU v7x, 32 devices: a whole 2x2x4 slice. The times are simulated.
32 devices in a mesh: rep: 4 (over z), tp: 8 (over y, x, core).
Axes of the slice: x: 2, y: 2, z: 4, core: 2. Of those that a mesh axis runs over, the one named last changes fastest.
Arguments:
- attn: bfloat16 [3072, 4096], P('rep', 'tp'), parts along dimension 0, may hold values from -6 to 6
- output_weight: bfloat16 [4096, 8192], P(None, 'tp'), may hold values from -0.09375 to 0.09375
- adapter_down_weight: bfloat16 [8, 64, 4096], P('tp'), may hold values from -0.09375 to 0.09375
- adapter_up_weight: bfloat16 [8, 64, 8192], P('tp'), may hold values from -0.75 to 0.75
- block_adapter_index: int32 [24], P('rep'), parts along dimension 0, may hold values from 0 to 7
- adapter_page_table: int32 [8], replicated, may hold values from 0 to 7, each once
Outputs:
- projected: bfloat16 [3072, 8192], P('rep', 'tp'), parts along dimension 0
There are 4 independent parts, one for each index of `rep`. A program takes and returns all parts, laid end to end along the dimension named above; an argument that names none is the same for every part. Nothing has to cross between parts.
Inputs may be any that keep to these rules, and one draw needn't show every extreme that they name: adapter_page_table is a permutation; adapter a is stored on tp device adapter_page_table[a] (each device holds exactly one adapter), and row adapter_page_table[a] of adapter_down_weight and adapter_up_weight holds it. `block_adapter_index`: the adapter used by all 128 tokens of a block.
All inputs are finite; a program needn't handle non-finite values.
Results may differ from a plain program's by a relative error of at most 0.0046.
Values may be sent and summed in bfloat16 or wider, within the bound.
A program may use at most 64 MiB of HBM per device.

v0:
```python
import jax
import jax.numpy as jnp
from jax import lax
from jax.sharding import PartitionSpec as P

adapter_scale = 2.0


def shards(
    attn,
    output_weight,
    adapter_down_weight,
    adapter_up_weight,
    block_adapter_index,
    adapter_page_table,
):
    tokens = attn.shape[0]
    blocks = block_adapter_index.shape[0]
    block_rows = tokens // blocks
    page_slot_count = adapter_down_weight.shape[0]
    pool_size = adapter_page_table.shape[0]
    width_out = output_weight.shape[1]
    position = lax.axis_index("tp")
    matches = block_adapter_index[:, None] == jnp.arange(pool_size, dtype=jnp.int32)[None, :]
    block_page_index = jnp.sum(jnp.where(matches, adapter_page_table[None, :], 0), axis=1)
    up_weight_columns = lax.all_to_all(
        adapter_up_weight, "tp", split_axis=2, concat_axis=0, tiled=True
    )
    block_up = up_weight_columns[block_page_index]
    shard_piece = lax.all_gather(attn, "tp", axis=1, tiled=True)
    base_output = jnp.dot(shard_piece, output_weight, preferred_element_type=jnp.float32)
    row_blocks = shard_piece.reshape(blocks, block_rows, shard_piece.shape[1])
    base_output, side_sum = (
        base_output,
        jnp.einsum(
            "btf,srf->bsrt", row_blocks, adapter_down_weight, preferred_element_type=jnp.float32
        ),
    )
    own_pages = position * page_slot_count + jnp.arange(page_slot_count, dtype=jnp.int32)
    owned = (block_page_index[:, None] == own_pages[None, :]).astype(jnp.float32)
    local_term = jnp.sum(owned[:, :, None, None] * side_sum, axis=1)
    shrunk = lax.psum(local_term.astype(jnp.bfloat16), "tp")
    adapter_output = jnp.einsum(
        "brt,brc->btc", shrunk, block_up, preferred_element_type=jnp.float32
    )
    adapter_output = adapter_output.reshape(tokens, width_out)
    return (base_output + adapter_scale * adapter_output).astype(jnp.bfloat16)


def solution(mesh):
    return jax.shard_map(
        shards,
        mesh=mesh,
        in_specs=(
            P("rep", "tp"),
            P(None, "tp"),
            P("tp", None, None),
            P("tp", None, None),
            P("rep"),
            P(),
        ),
        out_specs=P("rep", "tp"),
        check_vma=False,
    )
```

profile of v0, /device:TPU:0, one launch (start us, length us, event | category | flops | bytes accessed | tf_op | source)
XLA Modules:
  0.0 150.3 jit_solution(16534256131757500711)
XLA Ops:
  6.5 0.0 copy-start
  6.5 0.0 all-gather.2.cloned.1.call-start
  6.5 0.7 all-gather.2.cloned.1.call-update
  7.3 9.2 %copy.11 = bf16[1,64,8192]{1,0,2:T(2,128)(2,1)} copy(bf16[1,64,8192]{2,1,0:T(8,128)(2,1)} %param.9) | data formatting | bytes 2097152 | tf_op args[3]
  16.4 0.5 broadcast.42
  16.9 45.3 %reduce = bf16[8192,64]{1,0:T(8,128)(2,1)S(1)} reduce(bf16[8192,1,64]{2,1,0:T(2,128)(2,1)} %bitcast.36, bf16[]{:T(256)} %broadcast.42), dimensions={1}, to_apply=%bitcast.29.reduce_sub_computation | reduce | bytes 2097154
  62.2 0.0 copy-start.1
  62.2 0.0 copy-start.2
  62.2 2.7 %reshape.51 = bf16[8,2,32768]{2,1,0:T(2,128)(2,1)} reshape(bf16[8192,64]{1,0:T(8,128)(2,1)S(1)} %reduce) | data formatting | bytes 2097152
  64.9 5.2 %all-to-all-start = ((bf16[8,2,32768]{2,1,0:T(2,128)(2,1)}), bf16[8,2,32768]{2,1,0:T(2,128)(2,1)S(1)}, u32[]{:S(2)}, u32[]{:S(2)}) async-start(bf16[8,2,32768]{2,1,0:T(2,128)(2,1)} %reshape.51), calls=%async_computation | async-start | bytes 2097152 | tf_op jit(solution)/shard_map/all_to_all | solution.py:26
  70.1 0.2 all-reduce.2.cloned.1.call-start
  70.3 0.0 copy-done.1
  70.3 0.0 copy-done.2
  70.4 0.2 select_reduce_fusion
  70.6 0.0 all-gather.2.cloned.1.call-done
  70.6 0.0 copy-done
  70.6 5.5 %fusion.3 = bf16[6,64,128]{2,1,0:T(8,128)(2,1)} fusion(bf16[6,128,4096]{2,1,0:T(8,128)(2,1)} %bitcast.39, bf16[1,64,4096]{2,1,0:T(8,128)(2,1)S(1)} %copy-done, f32[6]{0:T(128)S(1)} %compare_convert_fusion), kind=kOutput, calls=%fused_computation.7 | convolution fusion | flops 402751488 | bytes 6914072 | tf_op jit(solution)/shard_map/btf,srf->bsrt/dot_general | solution.py:35
  76.0 0.0 all-reduce.2.cloned.1.call-update
  76.1 9.4 %all-to-all-done = bf16[8,2,32768]{2,1,0:T(2,128)(2,1)S(1)} async-done(((bf16[8,2,32768]{2,1,0:T(2,128)(2,1)}), bf16[8,2,32768]{2,1,0:T(2,128)(2,1)S(1)}, u32[]{:S(2)}, u32[]{:S(2)}) %all-to-all-start) | async-done | bytes 1048608 | tf_op jit(solution)/shard_map/all_to_all | solution.py:26
  85.5 4.3 %reshape.52 = bf16[8192,1,64]{2,1,0:T(2,128)(2,1)} reshape(bf16[8,2,32768]{2,1,0:T(2,128)(2,1)S(1)} %all-to-all-done) | data formatting | bytes 2097152
  89.9 2.5 %copy.16 = bf16[1,64,8192]{1,2,0:T(8,128)(2,1)S(1)} copy(bf16[1,64,8192]{1,0,2:T(2,128)(2,1)} %bitcast.37) | data formatting | bytes 2097152
  92.3 1.6 %copy.13 = bf16[1,64,8,1024]{3,1,2,0:T(8,128)(2,1)} copy(bf16[1,64,8,1024]{1,3,2,0:T(8,128)(2,1)S(1)} %bitcast.38) | data formatting | bytes 2097152 | tf_op jit(solution)/shard_map/all_to_all | solution.py:26
  93.9 1.8 %gather_fusion = bf16[6,64,1024]{2,1,0:T(8,128)(2,1)S(1)} fusion(bf16[8,64,1024]{2,1,0:T(8,128)(2,1)} %bitcast.40, s32[1024]{0:T(1024)S(1)} %pad_clamp_fusion), kind=kCustom, calls=%fused_computation | custom fusion | bytes 1572888 | tf_op jit(solution)/shard_map/gather | solution.py:29
  95.8 34.1 %all-reduce.2.cloned.1.call-done = bf16[6,64,128]{2,1,0:T(8,128)(2,1)} async-done(((bf16[6,64,128]{2,1,0:T(8,128)(2,1)}), bf16[6,64,128]{2,1,0:T(8,128)(2,1)}) %all-reduce.2.cloned.1.call-update) | async-done | bytes 98320 | tf_op jit(solution)/shard_map/psum | solution.py:42
  129.9 1.5 %convolution_multiply_fusion = f32[6,128,1024]{2,1,0:T(8,128)S(1)} fusion(bf16[6,64,128]{2,1,0:T(8,128)(2,1)} %all-reduce.2.cloned.1.call-done, bf16[6,64,1024]{2,1,0:T(8,128)(2,1)S(1)} %gather_fusion), kind=kOutput, calls=%fused_computation.3 | convolution fusion | flops 101449728 | bytes 4030464 | tf_op jit(solution)/shard_map/brt,brc->btc/dot_general | solution.py:43
  131.4 12.1 %fusion = bf16[768,1024]{1,0:T(8,128)(2,1)} fusion(f32[6,128,1024]{2,1,0:T(8,128)S(1)} %convolution_multiply_fusion, bf16[768,4096]{1,0:T(8,128)(2,1)} %all-gather.2.cloned.1.call-done, bf16[4096,1024]{1,0:T(8,128)(2,1)} %param.7), kind=kOutput, calls=%fused_computation.2 | convolution fusion | flops 6444023808 | bytes 19398656 | tf_op jit(solution)/shard_map/dot_general | solution.py:31
  (3 shorter events, 0.0 us)
Async XLA Ops:
  6.5 64.1 %copy-start = (bf16[1,64,4096]{2,1,0:T(8,128)(2,1)S(1)}, bf16[1,64,4096]{2,1,0:T(8,128)(2,1)}, u32[]{:S(2)}) copy-start(bf16[1,64,4096]{2,1,0:T(8,128)(2,1)} %param.8) | copy-start | bytes 1572868
  6.5 64.0 %all-gather.2.cloned.1.call-start = ((), (), s32[]{:S(2)}) async-start(), calls=%async_computation.1 | async-start | bytes 7077888 | tf_op jit(solution)/shard_map/all_gather | solution.py:30
  62.2 8.1 %copy-start.1 = (s32[8]{0:T(128)S(1)}, s32[8]{0:T(128)}, u32[]{:S(2)}) copy-start(s32[8]{0:T(128)} %param.11) | copy-start | bytes 100
  62.2 8.1 %copy-start.2 = (s32[6]{0:T(128)S(1)}, s32[6]{0:T(128)}, u32[]{:S(2)}) copy-start(s32[6]{0:T(128)} %param.10) | copy-start | bytes 76
  64.9 20.6 %all-to-all-start = ((bf16[8,2,32768]{2,1,0:T(2,128)(2,1)}), bf16[8,2,32768]{2,1,0:T(2,128)(2,1)S(1)}, u32[]{:S(2)}, u32[]{:S(2)}) async-start(bf16[8,2,32768]{2,1,0:T(2,128)(2,1)} %reshape.51), calls=%async_computation | async-start | bytes 2097152 | tf_op jit(solution)/shard_map/all_to_all | solution.py:26
  70.1 59.7 %all-reduce.2.cloned.1.call-start = ((), (), s32[]{:S(2)}) async-start(), calls=%async_computation.2 | async-start | bytes 196608 | tf_op jit(solution)/shard_map/psum | solution.py:42
Sparse Core Ops, SparseCore 0:
  9.2 49.2 all-gather.1
  76.2 53.6 all-reduce.1
where the time goes:
time: 151 us; the launch traced here: 150 us
  other arithmetic  45.5 us (30%)
  waiting for transfers between devices  44.3 us (29%)
  local copies, waits for them, and re-layouts  22.6 us (15%)
  matrix products  19.1 us (13%)
  between operations  13.5 us (9%)
  starting transfers between devices  5.45 us (4%)
    unnamed x1, other arithmetic  45.3 us
    psum x1, waiting for transfers between devices, shards(): shrunk = lax.psum(local_term.astype(jnp.bfloat16), 'tp')  34.1 us
    unnamed x11, local copies, waits for them, and re-layouts  19.2 us
    dot_general x1, matrix products, shards(): jnp.dot(shard_piece, output_weight, preferred_element_type=jnp.float32)  12.1 us
    all_to_all x1, waiting for transfers between devices, shards(): lax.all_to_all(adapter_up_weight, 'tp', split_axis=2, concat_axis=0, tile...  9.44 us
    dot_general x1, matrix products, shards(): jnp.einsum('btf,srf->bsrt', row_blocks, adapter_down_weight, preferred_el...  5.45 us
    all_to_all x1, starting transfers between devices, shards(): lax.all_to_all(adapter_up_weight, 'tp', split_axis=2, concat_axis=0, tile...  5.23 us
  transfers between devices with their start and end apart: 3, of which 2 were waited for; matrix products, arithmetic and copies ran while one was open for 49% of the time, Pallas kernels for 0%

commit v1 on v0

--- a/solution.py
+++ b/solution.py
@@ -39,7 +39,9 @@
     own_pages = position * page_slot_count + jnp.arange(page_slot_count, dtype=jnp.int32)
     owned = (block_page_index[:, None] == own_pages[None, :]).astype(jnp.float32)
     local_term = jnp.sum(owned[:, :, None, None] * side_sum, axis=1)
-    shrunk = lax.psum(local_term.astype(jnp.bfloat16), "tp")
+    block = local_term.astype(jnp.bfloat16)
+    pieces = lax.all_gather(block, "tp", axis=0, tiled=False)
+    shrunk = pieces.sum(axis=0)
     adapter_output = jnp.einsum(
         "brt,brc->btc", shrunk, block_up, preferred_element_type=jnp.float32
     )

time: 151 us -> 129 us (0.85)
  waiting for transfers between devices: 44.3 us -> 15.9 us
  blocking collectives: 0 us -> 9.62 us
  matrix products: 19.1 us -> 15.5 us
    psum x1 -> x0, waiting for transfers between devices: 34.1 us -> none  [shards(): shrunk = lax.psum(local_term.astype(jnp.bfloat16), 'tp')]
    all_gather x0 -> x1, blocking collectives: none -> 9.62 us  [shards(): pieces = lax.all_gather(block, 'tp', axis=0, tiled=False)]
    all_to_all x1, waiting for transfers between devices: 9.44 us -> 15.1 us  [shards(): lax.all_to_all(adapter_up_weight, 'tp', split_axis=2, concat_axis=0, tile...]
    dot_general x1, matrix products: 12.1 us -> 9.92 us  [shards(): jnp.dot(shard_piece, output_weight, preferred_element_type=jnp.float32)]
    unnamed x11 -> x15, local copies, waits for them, and re-layouts: 19.2 us -> 19.2 us
    unnamed x1 -> x2, other arithmetic: 45.3 us -> 45.3 us
  transfers between devices with their start and end apart: 3 -> 2, of which waited for: 2 -> 1; matrix products, arithmetic and copies ran while one was open for 49% -> 53% of each run, Pallas kernels for 0% -> 0%
where the time goes in v1:
time: 129 us; the launch traced here: 128 us
  other arithmetic  45.6 us (35%)
  local copies, waits for them, and re-layouts  22.6 us (18%)
  waiting for transfers between devices  15.9 us (12%)
  matrix products  15.5 us (12%)
  between operations  13.5 us (10%)
  blocking collectives  9.62 us (7%)
  starting transfers between devices  5.22 us (4%)
    unnamed x2, other arithmetic  45.3 us
    unnamed x15, local copies, waits for them, and re-layouts  19.2 us
    all_to_all x1, waiting for transfers between devices, shards(): lax.all_to_all(adapter_up_weight, 'tp', split_axis=2, concat_axis=0, tile...  15.1 us
    dot_general x1, matrix products, shards(): jnp.dot(shard_piece, output_weight, preferred_element_type=jnp.float32)  9.92 us
    all_gather x1, blocking collectives, shards(): pieces = lax.all_gather(block, 'tp', axis=0, tiled=False)  9.62 us
    all_to_all x1, starting transfers between devices, shards(): lax.all_to_all(adapter_up_weight, 'tp', split_axis=2, concat_axis=0, tile...  5.22 us
    dot_general x1, matrix products, shards(): jnp.einsum('btf,srf->bsrt', row_blocks, adapter_down_weight, preferred_el...  4.96 us
  transfers between devices with their start and end apart: 2, of which 1 were waited for; matrix products, arithmetic and copies ran while one was open for 53% of the time, Pallas kernels for 0%

profile of v1, /device:TPU:0, one launch (start us, length us, event | category | flops | bytes accessed | tf_op | source)
XLA Modules:
  0.0 127.9 jit_solution(10916704434097761115)
XLA Ops:
  6.5 0.0 copy-start
  6.5 0.0 all-gather.3.cloned.1.call-start
  6.5 0.7 all-gather.3.cloned.1.call-update
  7.3 9.2 %copy.13 = bf16[1,64,8192]{1,0,2:T(2,128)(2,1)} copy(bf16[1,64,8192]{2,1,0:T(8,128)(2,1)} %param.9) | data formatting | bytes 2097152 | tf_op args[3]
  16.4 0.5 broadcast.42
  17.0 45.3 %reduce.1 = bf16[8192,64]{1,0:T(8,128)(2,1)S(1)} reduce(bf16[8192,1,64]{2,1,0:T(2,128)(2,1)} %bitcast.39, bf16[]{:T(256)} %broadcast.42), dimensions={1}, to_apply=%bitcast.31.reduce_sub_computation | reduce | bytes 2097154
  62.2 0.0 copy-start.1
  62.2 0.0 copy-start.2
  62.2 2.7 %reshape.62 = bf16[8,2,32768]{2,1,0:T(2,128)(2,1)} reshape(bf16[8192,64]{1,0:T(8,128)(2,1)S(1)} %reduce.1) | data formatting | bytes 2097152
  64.9 5.2 %all-to-all-start = ((bf16[8,2,32768]{2,1,0:T(2,128)(2,1)}), bf16[8,2,32768]{2,1,0:T(2,128)(2,1)S(1)}, u32[]{:S(2)}, u32[]{:S(2)}) async-start(bf16[8,2,32768]{2,1,0:T(2,128)(2,1)} %reshape.62), calls=%async_computation | async-start | bytes 2097152 | tf_op jit(solution)/shard_map/all_to_all | solution.py:26
  70.1 0.0 copy-done.1
  70.1 0.0 copy-done.2
  70.1 0.2 select_reduce_fusion
  70.3 15.1 %all-to-all-done = bf16[8,2,32768]{2,1,0:T(2,128)(2,1)S(1)} async-done(((bf16[8,2,32768]{2,1,0:T(2,128)(2,1)}), bf16[8,2,32768]{2,1,0:T(2,128)(2,1)S(1)}, u32[]{:S(2)}, u32[]{:S(2)}) %all-to-all-start) | async-done | bytes 1048608 | tf_op jit(solution)/shard_map/all_to_all | solution.py:26
  85.5 4.3 %reshape.63 = bf16[8192,1,64]{2,1,0:T(2,128)(2,1)} reshape(bf16[8,2,32768]{2,1,0:T(2,128)(2,1)S(1)} %all-to-all-done) | data formatting | bytes 2097152
  89.8 2.5 %copy.18 = bf16[1,64,8192]{1,2,0:T(8,128)(2,1)S(1)} copy(bf16[1,64,8192]{1,0,2:T(2,128)(2,1)} %bitcast.40) | data formatting | bytes 2097152
  92.3 1.6 %copy.15 = bf16[1,64,8,1024]{3,1,2,0:T(8,128)(2,1)} copy(bf16[1,64,8,1024]{1,3,2,0:T(8,128)(2,1)S(1)} %bitcast.41) | data formatting | bytes 2097152 | tf_op jit(solution)/shard_map/all_to_all | solution.py:26
  93.9 1.8 %gather_fusion = bf16[6,64,1024]{2,1,0:T(8,128)(2,1)S(1)} fusion(bf16[8,64,1024]{2,1,0:T(8,128)(2,1)} %bitcast.45, s32[1024]{0:T(1024)S(1)} %pad_clamp_fusion), kind=kCustom, calls=%fused_computation | custom fusion | bytes 1572888 | tf_op jit(solution)/shard_map/gather | solution.py:29
  95.7 0.0 all-gather.3.cloned.1.call-done
  95.8 0.0 slice-start
  95.8 0.0 copy-done
  95.8 0.0 slice-start.1
  95.8 5.0 %fusion.3 = bf16[6,1,64,128]{3,2,1,0:T(8,128)(2,1)S(1)} fusion(bf16[6,128,4096]{2,1,0:T(8,128)(2,1)} %bitcast.42, bf16[1,64,4096]{2,1,0:T(8,128)(2,1)S(1)} %copy-done, f32[6]{0:T(128)S(1)} %compare_convert_fusion), kind=kOutput, calls=%fused_computation.7 | convolution fusion | flops 402751488 | bytes 6914072 | tf_op jit(solution)/shard_map/btf,srf->bsrt/dot_general | solution.py:35
  100.8 9.6 %all-gather = bf16[48,1,64,128]{3,2,1,0:T(8,128)(2,1)S(1)} all-gather(bf16[6,1,64,128]{3,2,1,0:T(8,128)(2,1)S(1)} %fusion.3), channel_id=2, replica_groups=mesh['rep'=4,'tp'=8] {'tp'}, dimensions={0}, use_global_device_ids=true | all-gather | bytes 884736 | tf_op jit(solution)/shard_map/all_gather | solution.py:43
  110.4 0.1 bitcast_reduce_fusion
  110.5 0.6 convolution_multiply_fusion
  111.1 0.0 slice-done
  111.1 0.0 slice-done.1
  111.2 9.9 %fusion = bf16[768,1024]{1,0:T(8,128)(2,1)} fusion(f32[6,128,1024]{2,1,0:T(8,128)S(1)} %convolution_multiply_fusion, bf16[768,4096]{1,0:T(8,128)(2,1)S(1)} %bitcast.44, bf16[4096,1024]{1,0:T(8,128)(2,1)} %param.7), kind=kOutput, calls=%fused_computation.2 | convolution fusion | flops 6444023808 | bytes 19398656 | tf_op jit(solution)/shard_map/dot_general | solution.py:31
  (4 shorter events, 0.0 us)
Async XLA Ops:
  6.5 89.3 %copy-start = (bf16[1,64,4096]{2,1,0:T(8,128)(2,1)S(1)}, bf16[1,64,4096]{2,1,0:T(8,128)(2,1)}, u32[]{:S(2)}) copy-start(bf16[1,64,4096]{2,1,0:T(8,128)(2,1)} %param.8) | copy-start | bytes 1572868
  6.5 89.2 %all-gather.3.cloned.1.call-start = ((), (), s32[]{:S(2)}) async-start(), calls=%async_computation.1 | async-start | bytes 7077888 | tf_op jit(solution)/shard_map/all_gather | solution.py:30
  62.2 7.9 %copy-start.1 = (s32[8]{0:T(128)S(1)}, s32[8]{0:T(128)}, u32[]{:S(2)}) copy-start(s32[8]{0:T(128)} %param.11) | copy-start | bytes 100
  62.2 7.9 %copy-start.2 = (s32[6]{0:T(128)S(1)}, s32[6]{0:T(128)}, u32[]{:S(2)}) copy-start(s32[6]{0:T(128)} %param.10) | copy-start | bytes 76
  64.9 20.6 %all-to-all-start = ((bf16[8,2,32768]{2,1,0:T(2,128)(2,1)}), bf16[8,2,32768]{2,1,0:T(2,128)(2,1)S(1)}, u32[]{:S(2)}, u32[]{:S(2)}) async-start(bf16[8,2,32768]{2,1,0:T(2,128)(2,1)} %reshape.62), calls=%async_computation | async-start | bytes 2097152 | tf_op jit(solution)/shard_map/all_to_all | solution.py:26
  95.8 15.4 %slice-start = ((s8[6291456]{0:T(1024)(128)(4,1)}), s8[4194304]{0:T(1024)(128)(4,1)S(1)}, s32[]{:S(2)}) async-start(s8[6291456]{0:T(1024)(128)(4,1)} %bitcast.43), calls=%async_computation.2 | async-start | bytes 8388608
  95.8 15.3 %slice-start.1 = ((s8[6291456]{0:T(1024)(128)(4,1)}), s8[2097152]{0:T(1024)(128)(4,1)S(1)}, s32[]{:S(2)}) async-start(s8[6291456]{0:T(1024)(128)(4,1)} %bitcast.43), calls=%async_computation.3 | async-start | bytes 4194304
Sparse Core Ops, SparseCore 0:
  9.2 49.2 all-gather.2
